TPU v7x, 32 devices: a whole 2x2x4 slice. The times are simulated.
32 devices in a mesh: lat: 16 (over z, y, x), lon: 2 (over core).
Axes of the slice: x: 2, y: 2, z: 4, core: 2. Of those that a mesh axis runs over, the one named last changes fastest.
Arguments:
- fields: bfloat16 [2048, 2, 1024], P('lat', 'lon'), may hold values from -6 to 6
- proj_x: bfloat16 [1024, 1024], P('lon'), may hold values from -0.1875 to 0.1875
- proj_z: bfloat16 [1024, 1024], P('lon'), may hold values from -0.1875 to 0.1875
- proj_bc: bfloat16 [1024, 128], P('lon'), may hold values from -0.1875 to 0.1875
- proj_dt: bfloat16 [1024, 16], P('lon'), may hold values from -1 to 1
- conv_x: float32 [4, 1024], replicated, may hold values from -3 to 3
- conv_bc: float32 [4, 128], replicated, may hold values from -3 to 3
- dt_bias: float32 [16], replicated, may hold values from -1 to 0.5
- log_rate: float32 [16], replicated, may hold values from -12 to -2.7
- norm_gain: float32 [1024], replicated, may hold values from 0.1 to 1.9
- proj_out: bfloat16 [1024, 1024], P('lon'), may hold values from -0.1875 to 0.1875
Outputs:
- mixer_out: bfloat16 [2048, 2, 1024], P('lat', 'lon')
All inputs are finite; a program needn't handle non-finite values.
Results may differ from a plain program's by a relative error of at most 0.012.
Values may be sent and summed in bfloat16 or wider, within the bound.
A program may use at most 64 MiB of HBM per device.

v0:
```python
import jax
import jax.numpy as jnp
from jax import lax
from jax.sharding import PartitionSpec as P

norm_epsilon = 1e-05
highest = lax.Precision.HIGHEST


def shifted(block, axis, distance):
    devices = range(lax.axis_size(axis))
    route = [(i - distance, i) for i in devices if i - distance in devices]
    return lax.ppermute(block, axis, route)


def partner_2(block, axis, apart):
    count = lax.axis_size(axis)
    route = []
    for low in range(count):
        high = low | 1 << apart
        if high != low and high < count:
            route += [(low, high), (high, low)]
    return lax.ppermute(block, axis, route)


def causal_conv(values, kernel):
    out_rows = values.shape[0] - kernel.shape[0] + 1
    acc_sum = jnp.zeros((out_rows,) + values.shape[1:], jnp.float32)
    for offset in range(kernel.shape[0]):
        acc_sum = acc_sum + kernel[offset] * values[offset : offset + out_rows]
    return jax.nn.silu(acc_sum).astype(jnp.bfloat16)


def combine(earlier_part, later_part):
    return (
        earlier_part[0] + later_part[0],
        jnp.exp(later_part[0])[..., None] * earlier_part[1] + later_part[1],
    )


def local(
    fields,
    proj_x,
    proj_z,
    proj_bc,
    proj_dt,
    conv_x,
    conv_bc,
    dt_bias,
    log_rate,
    norm_gain,
    proj_out,
):
    band_rows, band_cols, model_width = fields.shape
    margin = conv_x.shape[0] - 1
    head_count = log_rate.shape[0]
    inner_width = proj_x.shape[1]
    state_size = proj_bc.shape[1] // 2
    row_count = fields.shape[0]
    flat_rows = fields.reshape(row_count * band_cols, model_width)
    pieces = (
        lax.all_gather(proj_x, "lon", axis=0, tiled=True),
        lax.all_gather(proj_z, "lon", axis=0, tiled=True),
        lax.all_gather(proj_bc, "lon", axis=0, tiled=True),
        lax.all_gather(proj_dt, "lon", axis=0, tiled=True),
    )
    columns = flat_rows
    projected = tuple(
        (jnp.dot(columns, piece_rows, preferred_element_type=jnp.float32) for piece_rows in pieces)
    )
    inner_pre, gate_pre, bc_pre, dt_pre = [
        result_sum.astype(jnp.bfloat16).reshape(row_count, band_cols, -1)
        for result_sum in projected
    ]
    tail_rows = shifted((inner_pre[band_rows - margin :], bc_pre[band_rows - margin :]), "lat", 1)
    inner_ext = jnp.concatenate([tail_rows[0], inner_pre], 0)
    bc_ext = jnp.concatenate([tail_rows[1], bc_pre], 0)
    inner_act = causal_conv(inner_ext.astype(jnp.float32), conv_x)
    bc_act = causal_conv(bc_ext.astype(jnp.float32), conv_bc)
    step_dt = jax.nn.softplus(dt_pre.astype(jnp.float32) + dt_bias)
    log_step = -jnp.exp(log_rate) * step_dt
    head_inner = inner_act.astype(jnp.float32).reshape(band_rows, band_cols, head_count, -1)
    input_b = bc_act[..., :state_size].astype(jnp.float32)
    read_c = bc_act[..., state_size:].astype(jnp.float32)
    cumulative = jnp.cumsum(log_step, axis=0)
    causal = jnp.arange(band_rows)[:, None] >= jnp.arange(band_rows)[None, :]
    decay_gap = cumulative[:, None] - cumulative[None, :]
    decay = jnp.exp(jnp.where(causal[:, :, None, None], decay_gap, -jnp.inf))
    scores = jnp.einsum("tcn,scn->tsc", read_c, input_b, precision=highest)
    weights = decay * scores[:, :, :, None] * step_dt[None]
    diag_out = jnp.einsum("tsch,schp->tchp", weights, head_inner, precision=highest)
    band_total = cumulative[-1]
    end_weight = jnp.exp(band_total[None] - cumulative) * step_dt
    end_state = jnp.einsum("sch,scn,schp->chnp", end_weight, input_b, head_inner, precision=highest)
    states = end_state.reshape(band_cols, head_count, -1)
    position = lax.axis_index("lat")
    prefix = (jnp.zeros_like(band_total), jnp.zeros_like(states))
    running = (band_total, states)
    for bit_level in range(lax.axis_size("lat").bit_length() - 1):
        partner = partner_2((running[0], running[1]), "lat", bit_level)
        later_half = position // (1 << bit_level) % 2 == 1
        merged_low = combine(partner, running)
        merged_high = combine(running, partner)
        moved_prefix = combine(partner, prefix)
        prefix = (
            jnp.where(later_half, moved_prefix[0], prefix[0]),
            jnp.where(later_half, moved_prefix[1], prefix[1]),
        )
        running = (
            jnp.where(later_half, merged_low[0], merged_high[0]),
            jnp.where(later_half, merged_low[1], merged_high[1]),
        )
    incoming = prefix[1]
    incoming = incoming.reshape(band_cols, head_count, state_size, -1)
    state_out = (
        jnp.einsum("tcn,chnp->tchp", read_c, incoming, precision=highest)
        * jnp.exp(cumulative)[..., None]
    )
    mixed_heads = (diag_out + state_out).reshape(band_rows, band_cols, inner_width)
    gated_out = mixed_heads * jax.nn.silu(gate_pre.astype(jnp.float32))
    normed = (
        gated_out
        * lax.rsqrt(jnp.mean(gated_out * gated_out, -1, keepdims=True) + norm_epsilon)
        * norm_gain
    )
    hidden = normed.astype(jnp.bfloat16).reshape(band_rows * band_cols, inner_width)
    columns = hidden
    result = jnp.dot(
        columns,
        lax.all_gather(proj_out, "lon", axis=0, tiled=True),
        preferred_element_type=jnp.float32,
    )
    return result.astype(jnp.bfloat16).reshape(band_rows, band_cols, model_width)


def solution(mesh):
    return jax.shard_map(
        local,
        mesh=mesh,
        in_specs=(
            P("lat", "lon", None),
            P("lon", None),
            P("lon", None),
            P("lon", None),
            P("lon", None),
            P(),
            P(),
            P(),
            P(),
            P(),
            P("lon", None),
        ),
        out_specs=P("lat", "lon", None),
        check_vma=False,
    )
```

profile of v0, /device:TPU:0, one launch (start us, length us, event | category | flops | bytes accessed | tf_op | source)
XLA Modules:
  0.0 81.1 jit_solution(3935069047673425926)
XLA Ops:
  6.5 0.0 copy-start
  6.5 0.0 copy-start.3
  6.5 0.0 all-gather.4.cloned.1.call-start
  6.5 0.7 all-gather.4.cloned.1.call-update
  7.3 0.0 all-gather.6.cloned.1.call-start
  7.3 2.2 %all_gather.16 = bf16[1024,16]{0,1:T(8,128)(2,1)S(1)} all-gather(bf16[512,16]{0,1:T(8,128)(2,1)} %param.15), channel_id=1, replica_groups=mesh['lat'=16,'lon'=2] {'lon'}, dimensions={0}, use_global_device_ids=true | all-gather | bytes 49152 | tf_op jit(solution)/shard_map/all_gather | solution.py:65
  9.5 0.7 exponential_negate_fusion
  10.2 0.0 copy-done
  10.2 0.9 %compare_select_fusion = f32[128,16]{0,1:T(8,128)S(1)} fusion(bf16[1024,16]{0,1:T(8,128)(2,1)S(1)} %all_gather.16, bf16[128,1,1024]{2,0,1:T(8,128)(2,1)S(1)} %copy-done, f32[16]{0:T(128)} %param.18), kind=kOutput, calls=%fused_computation.69 | convolution fusion | flops 4212736 | bytes 303168 | tf_op jit(solution)/shard_map/dot_general | solution.py:69
  11.0 0.1 multiply_bitcast_fusion
  11.1 0.1 copy.21
  11.2 0.1 fusion.47
  11.3 2.9 %collective-permute-start.2 = (f32[1,16]{1,0:T(1,128)S(1)}, f32[1,16]{1,0:T(1,128)S(1)}, u32[]{:S(2)}, u32[]{:S(2)}) collective-permute-start(f32[1,16]{1,0:T(1,128)S(1)} %get-tuple-element.11), channel_id=1, source_target_pairs={{0,2},{2,0},{4,6},{6,4},{8,10},{10,8},{12,14},{14,12},{16,18},{18,... | collective-permute-start | bytes 200 | tf_op jit(solution)/shard_map/ppermute | solution.py:23
  14.2 2.2 %all_gather.17 = bf16[1024,128]{1,0:T(8,128)(2,1)S(1)} all-gather(bf16[512,128]{1,0:T(8,128)(2,1)} %param.14), channel_id=1, replica_groups=mesh['lat'=16,'lon'=2] {'lon'}, dimensions={0}, use_global_device_ids=true | all-gather | bytes 393216 | tf_op jit(solution)/shard_map/all_gather | solution.py:64
  16.4 0.2 convolution_convert_fusion.3
  16.7 1.9 %collective-permute-start.1 = (bf16[3,1,128]{2,0,1:T(4,128)(2,1)S(1)}, bf16[3,1,128]{2,0,1:T(4,128)(2,1)S(1)}, u32[]{:S(2)}, u32[]{:S(2)}) collective-permute-start(bf16[3,1,128]{2,0,1:T(4,128)(2,1)S(1)} %slice_bitcast_fusion.3), channel_id=1, source_target_pairs={{0,2},{2,4},{4,6},{6,8},{8,10},{10,12},{12,14},{14,16},{16,18},{18... | collective-permute-start | bytes 2312 | tf_op jit(solution)/shard_map/ppermute | solution.py:13
  18.6 0.0 all-gather.6.cloned.1.call-update
  18.6 0.0 all-gather.8.cloned.1.call-start
  18.7 0.1 copy.22
  18.8 0.0 copy-done.3
  18.8 0.0 copy-done.1
  18.8 0.1 bitcast_exponential_fusion
  18.9 0.0 collective-permute-done.2
  18.9 2.1 %collective-permute-start.3 = (f32[1,16]{1,0:T(1,128)S(1)}, f32[1,16]{1,0:T(1,128)S(1)}, u32[]{:S(2)}, u32[]{:S(2)}) collective-permute-start(f32[1,16]{1,0:T(1,128)S(1)} %get-tuple-element.10), channel_id=1, source_target_pairs={{0,4},{4,0},{2,6},{6,2},{8,12},{12,8},{10,14},{14,10},{16,20},{20,... | collective-permute-start | bytes 200 | tf_op jit(solution)/shard_map/ppermute | solution.py:23
  21.0 0.0 collective-permute-done.1
  21.1 0.1 multiply_convert_fusion.3
  21.1 1.1 %all-gather.4.cloned.1.call-done = bf16[1024,1024]{1,0:T(8,128)(2,1)} async-done(((bf16[512,1024]{1,0:T(8,128)(2,1)}), bf16[1024,1024]{1,0:T(8,128)(2,1)}) %all-gather.4.cloned.1.call-update) | async-done | bytes 2097168 | tf_op jit(solution)/shard_map/all_gather | solution.py:62
  22.2 2.0 %convolution_convert_fusion.2 = bf16[128,1024]{1,0:T(8,128)(2,1)S(1)} fusion(bf16[1024,1024]{1,0:T(8,128)(2,1)} %all-gather.4.cloned.1.call-done, bf16[128,1,1024]{2,0,1:T(8,128)(2,1)S(1)} %copy-done), kind=kOutput, calls=%fused_computation.7 | convolution fusion | flops 268566528 | bytes 2621440 | tf_op jit(solution)/shard_map/dot_general | solution.py:69
  24.3 3.6 %collective-permute-start = (bf16[3,1,1024]{2,0,1:T(4,128)(2,1)S(1)}, bf16[3,1,1024]{2,0,1:T(4,128)(2,1)S(1)}, u32[]{:S(2)}, u32[]{:S(2)}) collective-permute-start(bf16[3,1,1024]{2,0,1:T(4,128)(2,1)S(1)} %slice_bitcast_fusion.2), channel_id=1, source_target_pairs={{0,2},{2,4},{4,6},{6,8},{8,10},{10,12},{12,14},{14,16},{16,18},{18... | collective-permute-start | bytes 18440 | tf_op jit(solution)/shard_map/ppermute | solution.py:13
  27.9 0.1 copy.24
  28.0 1.3 %collective-permute-done = bf16[3,1,1024]{2,0,1:T(4,128)(2,1)S(1)} collective-permute-done((bf16[3,1,1024]{2,0,1:T(4,128)(2,1)S(1)}, bf16[3,1,1024]{2,0,1:T(4,128)(2,1)S(1)}, u32[]{:S(2)}, u32[]{:S(2)}) %collective-permute-start) | collective-permute-done | bytes 6176 | tf_op jit(solution)/shard_map/ppermute | solution.py:13
  29.3 0.1 maximum_convert_fusion
  29.3 0.3 multiply_convert_fusion.1
  29.7 0.2 copy.20
  29.9 0.5 fusion.14
  30.4 0.2 reshape.305
  30.6 2.3 %collective-permute-start.5 = (f32[1,16,4096]{2,1,0:T(8,128)S(1)}, f32[1,16,4096]{2,1,0:T(8,128)S(1)}, u32[]{:S(2)}, u32[]{:S(2)}) collective-permute-start(f32[1,16,4096]{2,1,0:T(8,128)S(1)} %reshape.305), channel_id=1, source_target_pairs={{0,2},{2,0},{4,6},{6,4},{8,10},{10,8},{12,14},{14,12},{16,18},{18,... | collective-permute-start | bytes 786440 | tf_op jit(solution)/shard_map/ppermute | solution.py:23
  32.9 0.0 collective-permute-done.3
  32.9 3.6 %collective-permute-start.4 = (f32[1,16]{1,0:T(1,128)S(1)}, f32[1,16]{1,0:T(1,128)S(1)}, u32[]{:S(2)}, u32[]{:S(2)}) collective-permute-start(f32[1,16]{1,0:T(1,128)S(1)} %get-tuple-element.8), channel_id=1, source_target_pairs={{0,8},{8,0},{2,10},{10,2},{4,12},{12,4},{6,14},{14,6},{16,24},{24,... | collective-permute-start | bytes 200 | tf_op jit(solution)/shard_map/ppermute | solution.py:23
  36.5 1.5 %collective-permute-done.4 = f32[1,16]{1,0:T(1,128)S(1)} collective-permute-done((f32[1,16]{1,0:T(1,128)S(1)}, f32[1,16]{1,0:T(1,128)S(1)}, u32[]{:S(2)}, u32[]{:S(2)}) %collective-permute-start.4) | collective-permute-done | bytes 96 | tf_op jit(solution)/shard_map/ppermute | solution.py:23
  38.1 0.5 collective-permute-done.5
  38.5 0.1 add_select_fusion.5
  38.7 2.7 %collective-permute-start.6 = (f32[1,16,4096]{2,1,0:T(8,128)S(1)}, f32[1,16,4096]{2,1,0:T(8,128)S(1)}, u32[]{:S(2)}, u32[]{:S(2)}) collective-permute-start(f32[1,16,4096]{2,1,0:T(8,128)S(1)} %add_select_fusion.5), channel_id=1, source_target_pairs={{0,4},{4,0},{2,6},{6,2},{8,12},{12,8},{10,14},{14,10},{16,20},{20,... | collective-permute-start | bytes 786440 | tf_op jit(solution)/shard_map/ppermute | solution.py:23
  41.4 4.4 %collective-permute-done.6 = f32[1,16,4096]{2,1,0:T(8,128)S(1)} collective-permute-done((f32[1,16,4096]{2,1,0:T(8,128)S(1)}, f32[1,16,4096]{2,1,0:T(8,128)S(1)}, u32[]{:S(2)}, u32[]{:S(2)}) %collective-permute-start.6) | collective-permute-done | bytes 262176 | tf_op jit(solution)/shard_map/ppermute | solution.py:23
  45.7 0.1 add_select_fusion.4
  45.9 3.7 %collective-permute-start.7 = (f32[1,16,4096]{2,1,0:T(8,128)S(1)}, f32[1,16,4096]{2,1,0:T(8,128)S(1)}, u32[]{:S(2)}, u32[]{:S(2)}) collective-permute-start(f32[1,16,4096]{2,1,0:T(8,128)S(1)} %add_select_fusion.4), channel_id=1, source_target_pairs={{0,8},{8,0},{2,10},{10,2},{4,12},{12,4},{6,14},{14,6},{16,24},{24,... | collective-permute-start | bytes 786440 | tf_op jit(solution)/shard_map/ppermute | solution.py:23
  49.5 0.0 all-gather.8.cloned.1.call-update
  49.6 6.6 %collective-permute-done.7 = f32[1,16,4096]{2,1,0:T(8,128)S(1)} collective-permute-done((f32[1,16,4096]{2,1,0:T(8,128)S(1)}, f32[1,16,4096]{2,1,0:T(8,128)S(1)}, u32[]{:S(2)}, u32[]{:S(2)}) %collective-permute-start.7) | collective-permute-done | bytes 262176 | tf_op jit(solution)/shard_map/ppermute | solution.py:23
  56.2 0.1 add_select_fusion.3
  56.4 3.4 %collective-permute-start.8 = (f32[1,16,4096]{2,1,0:T(8,128)S(1)}, f32[1,16,4096]{2,1,0:T(8,128)S(1)}, u32[]{:S(2)}, u32[]{:S(2)}) collective-permute-start(f32[1,16,4096]{2,1,0:T(8,128)S(1)} %add_select_fusion.3), channel_id=1, source_target_pairs={{0,16},{16,0},{2,18},{18,2},{4,20},{20,4},{6,22},{22,6},{8,24},{24... | collective-permute-start | bytes 786440 | tf_op jit(solution)/shard_map/ppermute | solution.py:23
  59.8 0.2 convolution_bitcast_fusion.2
  60.0 0.1 copy.23
  60.1 6.8 %collective-permute-done.8 = f32[1,16,4096]{2,1,0:T(8,128)S(1)} collective-permute-done((f32[1,16,4096]{2,1,0:T(8,128)S(1)}, f32[1,16,4096]{2,1,0:T(8,128)S(1)}, u32[]{:S(2)}, u32[]{:S(2)}) %collective-permute-start.8) | collective-permute-done | bytes 262176 | tf_op jit(solution)/shard_map/ppermute | solution.py:23
  66.9 0.2 add_select_fusion
  67.1 0.2 reshape.306
  67.3 0.6 fusion.1
  68.0 1.3 %fusion = f32[128,1,16,64]{0,3,2,1:T(8,128)S(1)} fusion(f32[128,1,16,64]{0,3,2,1:T(8,128)S(1)} %fusion.1, bf16[128,16,64]{0,2,1:T(8,128)(2,1)S(1)} %bitcast.106, f32[128,16]{0,1:T(8,128)S(1)} %compare_select_fusion, f32[128,128]{1,0:T(8,128)S(1)} %copy.23, f32[128,16]{0,1:T(8,128)S(1)} %bitcast.109, pred[128,128]{1,0:T(8,128)(4,1)S(1)} %iota_compare_fusion), kind=kOutput, calls=%fused_computation.2 | convolution fusion | flops 202506240 | bytes 1409024 | tf_op jit(solution)/shard_map/tsch,schp->tchp/dot_general | solution.py:91
  69.3 0.2 copy.27
  69.5 0.0 copy-start.2
  69.5 0.0 all-gather.6.cloned.1.call-done
  69.5 2.2 %multiply_reduce_fusion = (f32[128]{0:T(128)S(1)}, f32[128,1024]{1,0:T(8,128)S(1)}) fusion(f32[128,1024]{1,0:T(8,128)S(1)} %copy.27, bf16[1024,1024]{1,0:T(8,128)(2,1)} %all-gather.6.cloned.1.call-done, bf16[128,1,1024]{2,0,1:T(8,128)(2,1)S(1)} %copy-done), kind=kOutput, calls=%fused_computation.27 | convolution fusion | flops 269614976 | bytes 3408384 | tf_op jit(solution)/shard_map/dot_general | solution.py:69
  71.7 0.0 all-gather.8.cloned.1.call-done
  71.7 0.0 copy-done.2
  71.7 2.8 %fusion.3 = bf16[128,1,1024]{2,0,1:T(8,128)(2,1)} fusion(bf16[1024,1024]{1,0:T(8,128)(2,1)} %all-gather.8.cloned.1.call-done, f32[128,1024]{1,0:T(8,128)S(1)} %get-tuple-element.28, f32[1024]{0:T(1024)S(1)} %copy-done.2, f32[128]{0:T(128)S(1)} %add_rsqrt_fusion), kind=kOutput, calls=%fused_computation.8 | convolution fusion | flops 268959744 | bytes 2888192 | tf_op jit(solution)/shard_map/dot_general | solution.py:128
  (15 shorter events, 0.1 us)
Async XLA Ops:
  6.5 3.6 %copy-start = (bf16[128,1,1024]{2,0,1:T(8,128)(2,1)S(1)}, bf16[128,1,1024]{2,0,1:T(8,128)(2,1)}, u32[]{:S(2)}) copy-start(bf16[128,1,1024]{2,0,1:T(8,128)(2,1)} %param.11) | copy-start | bytes 786436
  6.5 12.2 %copy-start.3 = (f32[4,128]{1,0:T(4,128)S(1)}, f32[4,128]{1,0:T(4,128)}, u32[]{:S(2)}) copy-start(f32[4,128]{1,0:T(4,128)} %param.17) | copy-start | bytes 6148
  6.5 12.3 %copy-start.1 = (f32[4,1024]{1,0:T(4,128)S(1)}, f32[4,1024]{1,0:T(4,128)}, u32[]{:S(2)}) copy-start(f32[4,1024]{1,0:T(4,128)} %param.16) | copy-start | bytes 49156
  6.5 15.7 %all-gather.4.cloned.1.call-start = ((), (), s32[]{:S(2)}) async-start(), calls=%async_computation | async-start | bytes 3145728 | tf_op jit(solution)/shard_map/all_gather | solution.py:62
  7.3 62.2 %all-gather.6.cloned.1.call-start = ((), (), s32[]{:S(2)}) async-start(), calls=%async_computation.1 | async-start | bytes 3145728 | tf_op jit(solution)/shard_map/all_gather | solution.py:63
  11.3 7.6 %collective-permute-start.2 = (f32[1,16]{1,0:T(1,128)S(1)}, f32[1,16]{1,0:T(1,128)S(1)}, u32[]{:S(2)}, u32[]{:S(2)}) collective-permute-start(f32[1,16]{1,0:T(1,128)S(1)} %get-tuple-element.11), channel_id=1, source_target_pairs={{0,2},{2,0},{4,6},{6,4},{8,10},{10,8},{12,14},{14,12},{16,18},{18,... | collective-permute-start | bytes 200 | tf_op jit(solution)/shard_map/ppermute | solution.py:23
  16.7 4.4 %collective-permute-start.1 = (bf16[3,1,128]{2,0,1:T(4,128)(2,1)S(1)}, bf16[3,1,128]{2,0,1:T(4,128)(2,1)S(1)}, u32[]{:S(2)}, u32[]{:S(2)}) collective-permute-start(bf16[3,1,128]{2,0,1:T(4,128)(2,1)S(1)} %slice_bitcast_fusion.3), channel_id=1, source_target_pairs={{0,2},{2,4},{4,6},{6,8},{8,10},{10,12},{12,14},{14,16},{16,18},{18... | collective-permute-start | bytes 2312 | tf_op jit(solution)/shard_map/ppermute | solution.py:13
  18.6 53.1 %all-gather.8.cloned.1.call-start = ((), (), s32[]{:S(2)}) async-start(), calls=%async_computation.2 | async-start | bytes 3145728 | tf_op jit(solution)/shard_map/all_gather | solution.py:130
  18.9 14.0 %collective-permute-start.3 = (f32[1,16]{1,0:T(1,128)S(1)}, f32[1,16]{1,0:T(1,128)S(1)}, u32[]{:S(2)}, u32[]{:S(2)}) collective-permute-start(f32[1,16]{1,0:T(1,128)S(1)} %get-tuple-element.10), channel_id=1, source_target_pairs={{0,4},{4,0},{2,6},{6,2},{8,12},{12,8},{10,14},{14,10},{16,20},{20,... | collective-permute-start | bytes 200 | tf_op jit(solution)/shard_map/ppermute | solution.py:23
  24.3 5.0 %collective-permute-start = (bf16[3,1,1024]{2,0,1:T(4,128)(2,1)S(1)}, bf16[3,1,1024]{2,0,1:T(4,128)(2,1)S(1)}, u32[]{:S(2)}, u32[]{:S(2)}) collective-permute-start(bf16[3,1,1024]{2,0,1:T(4,128)(2,1)S(1)} %slice_bitcast_fusion.2), channel_id=1, source_target_pairs={{0,2},{2,4},{4,6},{6,8},{8,10},{10,12},{12,14},{14,16},{16,18},{18... | collective-permute-start | bytes 18440 | tf_op jit(solution)/shard_map/ppermute | solution.py:13
  30.6 8.0 %collective-permute-start.5 = (f32[1,16,4096]{2,1,0:T(8,128)S(1)}, f32[1,16,4096]{2,1,0:T(8,128)S(1)}, u32[]{:S(2)}, u32[]{:S(2)}) collective-permute-start(f32[1,16,4096]{2,1,0:T(8,128)S(1)} %reshape.305), channel_id=1, source_target_pairs={{0,2},{2,0},{4,6},{6,4},{8,10},{10,8},{12,14},{14,12},{16,18},{18,... | collective-permute-start | bytes 786440 | tf_op jit(solution)/shard_map/ppermute | solution.py:23
  32.9 5.1 %collective-permute-start.4 = (f32[1,16]{1,0:T(1,128)S(1)}, f32[1,16]{1,0:T(1,128)S(1)}, u32[]{:S(2)}, u32[]{:S(2)}) collective-permute-start(f32[1,16]{1,0:T(1,128)S(1)} %get-tuple-element.8), channel_id=1, source_target_pairs={{0,8},{8,0},{2,10},{10,2},{4,12},{12,4},{6,14},{14,6},{16,24},{24,... | collective-permute-start | bytes 200 | tf_op jit(solution)/shard_map/ppermute | solution.py:23
  38.7 7.1 %collective-permute-start.6 = (f32[1,16,4096]{2,1,0:T(8,128)S(1)}, f32[1,16,4096]{2,1,0:T(8,128)S(1)}, u32[]{:S(2)}, u32[]{:S(2)}) collective-permute-start(f32[1,16,4096]{2,1,0:T(8,128)S(1)} %add_select_fusion.5), channel_id=1, source_target_pairs={{0,4},{4,0},{2,6},{6,2},{8,12},{12,8},{10,14},{14,10},{16,20},{20,... | collective-permute-start | bytes 786440 | tf_op jit(solution)/shard_map/ppermute | solution.py:23
  45.9 10.4 %collective-permute-start.7 = (f32[1,16,4096]{2,1,0:T(8,128)S(1)}, f32[1,16,4096]{2,1,0:T(8,128)S(1)}, u32[]{:S(2)}, u32[]{:S(2)}) collective-permute-start(f32[1,16,4096]{2,1,0:T(8,128)S(1)} %add_select_fusion.4), channel_id=1, source_target_pairs={{0,8},{8,0},{2,10},{10,2},{4,12},{12,4},{6,14},{14,6},{16,24},{24,... | collective-permute-start | bytes 786440 | tf_op jit(solution)/shard_map/ppermute | solution.py:23
  56.4 10.6 %collective-permute-start.8 = (f32[1,16,4096]{2,1,0:T(8,128)S(1)}, f32[1,16,4096]{2,1,0:T(8,128)S(1)}, u32[]{:S(2)}, u32[]{:S(2)}) collective-permute-start(f32[1,16,4096]{2,1,0:T(8,128)S(1)} %add_select_fusion.3), channel_id=1, source_target_pairs={{0,16},{16,0},{2,18},{18,2},{4,20},{20,4},{6,22},{22,6},{8,24},{24... | collective-permute-start | bytes 786440 | tf_op jit(solution)/shard_map/ppermute | solution.py:23
  69.5 2.3 %copy-start.2 = (f32[1024]{0:T(1024)S(1)}, f32[1024]{0:T(1024)}, u32[]{:S(2)}) copy-start(f32[1024]{0:T(1024)} %param.20) | copy-start | bytes 12292
Sparse Core Ops, SparseCore 0:
  8.9 13.2 all-gather.3
  23.8 11.7 all-gather.5
  49.7 8.9 all-gather.7
where the time goes:
time: 81.4 us; the launch traced here: 81.1 us
  starting transfers between devices  26.3 us (32%)
  waiting for transfers between devices  23 us (28%)
  between operations  13.4 us (16%)
  matrix products  10.8 us (13%)
  blocking collectives  4.38 us (5%)
  other arithmetic  1.99 us (2%)
  local copies, waits for them, and re-layouts  1.17 us (1%)
    ppermute x7, starting transfers between devices, partner_2(): return lax.ppermute(block, axis, route)  20.7 us
    ppermute x7, waiting for transfers between devices, partner_2(): return lax.ppermute(block, axis, route)  19.9 us
    ppermute x2, starting transfers between devices, shifted(): return lax.ppermute(block, axis, route)  5.56 us
    dot_general x4, matrix products, local(): jnp.dot(columns, piece_rows, preferred_element_type=jnp.float32)  5.28 us
    dot_general x1, matrix products, local(): jnp.dot(columns, lax.all_gather(proj_out, 'lon', axis=0, tiled=True), pre...  2.81 us
    all_gather x1, blocking collectives, local(): lax.all_gather(proj_bc, 'lon', axis=0, tiled=True)  2.19 us
    all_gather x1, blocking collectives, local(): lax.all_gather(proj_dt, 'lon', axis=0, tiled=True)  2.19 us
  transfers between devices with their start and end apart: 12, of which 7 were waited for; matrix products, arithmetic and copies ran while one was open for 14% of the time, Pallas kernels for 0%

commit v1 on v0

v1 whole, which is shorter than its diff:
```python
import functools

import jax
import jax.numpy as jnp
from jax import lax
from jax.experimental import pallas as pl
from jax.experimental.pallas import tpu as pltpu
from jax.sharding import PartitionSpec as P

norm_epsilon = 1e-05
LANES = 128
HALO = 16
f32 = jnp.float32
bf16 = jnp.bfloat16
highest = lax.Precision.HIGHEST


def silu(v):
    return v / (1.0 + jnp.exp(-v))


def expand(values, spread):
    high = values.astype(bf16)
    low = (values - high.astype(f32)).astype(bf16)
    return jnp.dot(high, spread, preferred_element_type=f32) + jnp.dot(
        low, spread, preferred_element_type=f32
    )


def kernel(
    n_lat,
    n_lon,
    heads,
    fields,
    wx,
    wz,
    wbc,
    wdt,
    wo,
    cx,
    cbc,
    dtb,
    lrate,
    gain,
    out,
    fbuf,
    bx,
    bz,
    bbc,
    bdt,
    bo,
    accx,
    accz,
    accbc,
    accdt,
    prm,
    act,
    diag,
    dec,
    tbuf,
    trecv,
    sbuf,
    srecv,
    pbuf,
    precv,
    local_sem,
    lon_send,
    lon_recv,
    halo_send,
    halo_recv,
    t_send,
    t_recv,
    s_send,
    s_recv,
    p_send,
    p_recv,
):
    rows, width = fields.shape
    inner = wx.shape[1]
    state = wbc.shape[1] // 2
    taps = cx.shape[0]
    kr = wx.shape[0]
    head_dim = inner // heads
    blocks = inner // LANES
    per_block = LANES // head_dim
    split = n_lat // blocks
    piece = state // split
    me = lax.axis_index("lat")
    col = lax.axis_index("lon")

    barrier = pltpu.get_barrier_semaphore()
    for k in range(1, n_lon):
        pl.semaphore_signal(barrier, inc=1, device_id={"lon": lax.rem(col + k, n_lon)})

    def greet(k, carry):
        pl.semaphore_signal(barrier, inc=1, device_id={"lat": lax.rem(me + k, n_lat)})
        return carry

    lax.fori_loop(1, n_lat, greet, 0)

    weights = ((wbc, bbc), (wdt, bdt), (wx, bx), (wz, bz), (wo, bo))
    own = [pltpu.make_async_copy(fields, fbuf.at[pl.ds(HALO, rows)], local_sem.at[5])]
    for i, (src, dst) in enumerate(weights):
        own.append(pltpu.make_async_copy(src, dst.at[col], local_sem.at[i]))
    for c in own:
        c.start()
    pl.semaphore_wait(barrier, n_lat - 1 + n_lon - 1)

    halo = pltpu.make_async_remote_copy(
        src_ref=fields.at[pl.ds(rows - HALO, HALO)],
        dst_ref=fbuf.at[pl.ds(0, HALO)],
        send_sem=halo_send,
        recv_sem=halo_recv,
        device_id={"lat": lax.rem(me + 1, n_lat)},
    )
    halo.start()

    def lon_copy(i, k):
        src, dst = weights[i]
        return pltpu.make_async_remote_copy(
            src_ref=src,
            dst_ref=dst.at[col],
            send_sem=lon_send.at[i, k],
            recv_sem=lon_recv.at[i, k],
            device_id={"lon": lax.rem(col + k, n_lon)},
        )

    for i in range(5):
        for k in range(1, n_lon):
            lon_copy(i, k).start()

    def part(k):
        source = lax.rem(col + n_lon - k, n_lon)
        return source, pl.ds(pl.multiple_of(source * kr, LANES), kr)

    def arrived(i, k):
        if k > 0:
            lon_copy(i, k).wait_recv()

    for c in own:
        c.wait()
    halo.wait_recv()
    keep = jnp.where(me > 0, 1.0, 0.0).astype(bf16)
    fbuf[0:HALO, :] = fbuf[0:HALO, :] * keep

    def accumulate(k, buf, acc, first_row, step):
        source, columns = part(k)
        lhs = fbuf[first_row:, columns]
        total = buf.shape[2]
        for start in range(0, total, step):
            size = min(step, total - start)
            term = jnp.dot(lhs, buf[source, :, start : start + size], preferred_element_type=f32)
            if k > 0:
                term = term + acc[:, start : start + size]
            if k == n_lon - 1:
                term = term.astype(bf16).astype(f32)
            acc[:, start : start + size] = term

    accumulate(0, bbc, accbc, 0, 256)
    accumulate(0, bdt, accdt, HALO, 256)
    accumulate(0, bx, accx, 0, 256)

    for k in range(1, n_lon):
        arrived(0, k)
        accumulate(k, bbc, accbc, 0, 256)
    for k in range(1, n_lon):
        arrived(1, k)
        accumulate(k, bdt, accdt, HALO, 256)

    def conv(acc, kernel_ref, start, size):
        total = None
        for k in range(taps):
            first = HALO - taps + 1 + k
            term = kernel_ref[k : k + 1, start : start + size] * acc[
                first : first + rows, start : start + size
            ]
            total = term if total is None else total + term
        return silu(total)

    bc_act = conv(accbc, cbc, 0, 2 * state)
    lane = lax.broadcasted_iota(jnp.int32, (rows, 2 * state), 1)
    bc16 = bc_act.astype(bf16)
    bc_f = bc16.astype(f32)
    read = pltpu.roll(bc_f, state, 1).astype(bf16)
    b_only = jnp.where(lane < state, bc_f, 0.0).astype(bf16)
    bc_t = bc_f.T.astype(bf16)

    prm[...] = jnp.zeros_like(prm)
    prm[0:1, 0:heads] = dtb[...]
    prm[1:2, 0:heads] = lrate[...]
    dec[0] = jnp.zeros((rows, LANES), f32)
    dec[0, :, 0:heads] = accdt[...]
    pre = dec[0] + prm[0:1, :]
    step_dt = jnp.maximum(pre, 0.0) + jnp.log1p(jnp.exp(-jnp.abs(pre)))
    log_step = -jnp.exp(prm[1:2, :]) * step_dt
    t_idx = lax.broadcasted_iota(jnp.int32, (rows, rows), 0)
    s_idx = lax.broadcasted_iota(jnp.int32, (rows, rows), 1)
    causal = t_idx >= s_idx
    cum = jnp.dot(
        jnp.where(causal, 1.0, 0.0), log_step, precision=highest, preferred_element_type=f32
    )
    dec[0] = cum
    dec[1] = cum.T
    dec[2] = step_dt.T
    band_total = cum[rows - 1 : rows, :]
    spread = jnp.where(
        lax.broadcasted_iota(jnp.int32, (LANES, inner), 1) // head_dim
        == lax.broadcasted_iota(jnp.int32, (LANES, inner), 0),
        1.0,
        0.0,
    ).astype(bf16)
    band_decay = expand(jnp.broadcast_to(jnp.exp(band_total), (8, LANES)), spread)
    for j in range(n_lat):
        c = j % blocks
        tbuf[j] = band_decay[:, c * LANES : (c + 1) * LANES]
    trecv[me] = tbuf[me]

    def exchange(k, buf, dst, send, recv):
        to = lax.rem(me + k, n_lat)
        return pltpu.make_async_remote_copy(
            src_ref=buf.at[to],
            dst_ref=dst.at[me],
            send_sem=send.at[to],
            recv_sem=recv.at[me],
            device_id={"lat": to},
        )

    def incoming(source, buf, dst, send, recv):
        return pltpu.make_async_remote_copy(
            src_ref=buf.at[source],
            dst_ref=dst.at[source],
            send_sem=send.at[source],
            recv_sem=recv.at[source],
            device_id={"lat": source},
        )

    def send_t(k, carry):
        exchange(k, tbuf, trecv, t_send, t_recv).start()
        return carry

    lax.fori_loop(1, n_lat, send_t, 0)

    scores = lax.dot_general(
        read, b_only, (((1,), (1,)), ((), ())), preferred_element_type=f32
    )
    end_weight = expand(jnp.exp(band_total - cum) * step_dt, spread)

    for k in range(1, n_lon):
        arrived(2, k)
        accumulate(k, bx, accx, 0, 256)
    for c in range(blocks):
        lanes = slice(c * LANES, (c + 1) * LANES)
        block = conv(accx, cx, c * LANES, LANES).astype(bf16)
        act[:, lanes] = block
        weighted = (block.astype(f32) * end_weight[:, lanes]).astype(bf16)
        end_state = jnp.dot(bc_t, weighted, preferred_element_type=f32)
        for r in range(split):
            sbuf[r * blocks + c] = end_state[r * piece : (r + 1) * piece, :].astype(bf16)
    srecv[me] = sbuf[me]

    def send_s(k, carry):
        exchange(k, sbuf, srecv, s_send, s_recv).start()
        return carry

    lax.fori_loop(1, n_lat, send_s, 0)

    half = lax.broadcasted_iota(jnp.int32, (rows, LANES), 1) // head_dim
    for c in range(blocks):
        lanes = slice(c * LANES, (c + 1) * LANES)
        mixed = None
        for g in range(per_block):
            h = c * per_block + g
            gap = dec[0, :, h : h + 1] - dec[1, h : h + 1, :]
            decay = jnp.exp(jnp.where(causal, gap, -jnp.inf))
            mix = (decay * scores * dec[2, h : h + 1, :]).astype(bf16)
            term = jnp.dot(mix, act[:, lanes], preferred_element_type=f32)
            mixed = term if mixed is None else jnp.where(half == g, term, mixed)
        diag[:, lanes] = mixed
    start_decay = jnp.exp(cum)

    carried = jnp.zeros((piece, LANES), f32)
    for d in range(n_lat):

        @pl.when(me != d)
        def _():
            incoming(d, tbuf, trecv, t_send, t_recv).wait_recv()
            incoming(d, sbuf, srecv, s_send, s_recv).wait_recv()

        pbuf[d] = carried.astype(bf16)
        carried = trecv[d][0:1, :] * carried + srecv[d].astype(f32)
    precv[me] = pbuf[me]

    def send_p(k, carry):
        exchange(k, pbuf, precv, p_send, p_recv).start()
        return carry

    lax.fori_loop(1, n_lat, send_p, 0)

    accumulate(0, bz, accz, HALO, 256)
    for k in range(1, n_lon):
        arrived(3, k)
        accumulate(k, bz, accz, HALO, 256)
    for c in range(blocks):
        lanes = slice(c * LANES, (c + 1) * LANES)
        accz[:, lanes] = silu(accz[:, lanes])
        accx[0:rows, lanes] = expand(start_decay, spread[:, lanes])
    for k in range(1, n_lon):
        arrived(4, k)

    def take_p(k, carry):
        incoming(lax.rem(me + k, n_lat), pbuf, precv, p_send, p_recv).wait_recv()
        return carry

    lax.fori_loop(1, n_lat, take_p, 0)

    square = jnp.zeros((rows, LANES), f32)
    for c in range(blocks):
        lanes = slice(c * LANES, (c + 1) * LANES)
        prefix = jnp.concatenate([precv[r * blocks + c] for r in range(split)], axis=0)
        lower = jnp.concatenate([jnp.zeros_like(prefix), prefix], axis=0)
        y = jnp.dot(bc16, lower, preferred_element_type=f32) * accx[0:rows, lanes] + diag[:, lanes]
        gated = y * accz[:, lanes]
        diag[:, lanes] = gated
        square = square + gated * gated
    mean = jnp.sum(square, axis=1, keepdims=True) * (1.0 / inner)
    scale = lax.rsqrt(mean + norm_epsilon)
    for c in range(blocks):
        lanes = slice(c * LANES, (c + 1) * LANES)
        act[:, lanes] = (diag[:, lanes] * scale * gain[:, lanes]).astype(bf16)
    for start in range(0, width, 256):
        total = None
        for s in range(n_lon):
            term = jnp.dot(
                act[:, s * kr : (s + 1) * kr],
                bo[s, :, start : start + 256],
                preferred_element_type=f32,
            )
            total = term if total is None else total + term
        out[:, start : start + 256] = total.astype(bf16)

    halo.wait_send()
    for i in range(5):
        for k in range(1, n_lon):
            lon_copy(i, k).wait_send()

    def drain(k, carry):
        exchange(k, tbuf, trecv, t_send, t_recv).wait_send()
        exchange(k, sbuf, srecv, s_send, s_recv).wait_send()
        exchange(k, pbuf, precv, p_send, p_recv).wait_send()
        return carry

    lax.fori_loop(1, n_lat, drain, 0)


def local(
    n_lat,
    n_lon,
    fields,
    proj_x,
    proj_z,
    proj_bc,
    proj_dt,
    conv_x,
    conv_bc,
    dt_bias,
    log_rate,
    norm_gain,
    proj_out,
):
    rows, cols, width = fields.shape
    heads = log_rate.shape[0]
    kr, inner = proj_x.shape
    state = proj_bc.shape[1] // 2
    piece = state * inner // LANES // n_lat
    any_spec = pl.BlockSpec(memory_space=pl.ANY)
    vmem = pl.BlockSpec(memory_space=pltpu.VMEM)
    dma = pltpu.SemaphoreType.DMA
    out = pl.pallas_call(
        functools.partial(kernel, n_lat, n_lon, heads),
        out_shape=jax.ShapeDtypeStruct((rows * cols, width), bf16),
        in_specs=[any_spec] * 6 + [vmem] * 5,
        out_specs=vmem,
        scratch_shapes=[
            pltpu.VMEM((HALO + rows, width), bf16),
            pltpu.VMEM((n_lon, kr, inner), bf16),
            pltpu.VMEM((n_lon, kr, inner), bf16),
            pltpu.VMEM((n_lon, kr, 2 * state), bf16),
            pltpu.VMEM((n_lon, kr, heads), bf16),
            pltpu.VMEM((n_lon,) + proj_out.shape, bf16),
            pltpu.VMEM((HALO + rows, inner), f32),
            pltpu.VMEM((rows, inner), f32),
            pltpu.VMEM((HALO + rows, 2 * state), f32),
            pltpu.VMEM((rows, heads), f32),
            pltpu.VMEM((8, LANES), f32),
            pltpu.VMEM((rows, inner), bf16),
            pltpu.VMEM((rows, inner), f32),
            pltpu.VMEM((3, rows, LANES), f32),
            pltpu.VMEM((n_lat, 8, LANES), f32),
            pltpu.VMEM((n_lat, 8, LANES), f32),
            pltpu.VMEM((n_lat, piece, LANES), bf16),
            pltpu.VMEM((n_lat, piece, LANES), bf16),
            pltpu.VMEM((n_lat, piece, LANES), bf16),
            pltpu.VMEM((n_lat, piece, LANES), bf16),
            dma((6,)),
            dma((5, n_lon)),
            dma((5, n_lon)),
            dma,
            dma,
        ]
        + [dma((n_lat,))] * 6,
        compiler_params=pltpu.CompilerParams(
            collective_id=0, has_side_effects=True, vmem_limit_bytes=56 * 1024 * 1024
        ),
    )(
        fields.reshape(rows * cols, width),
        proj_x,
        proj_z,
        proj_bc,
        proj_dt,
        proj_out,
        conv_x,
        conv_bc,
        dt_bias.reshape(1, -1),
        log_rate.reshape(1, -1),
        norm_gain.reshape(1, -1),
    )
    return out.reshape(rows, cols, width)


def solution(mesh):
    rows = P("lon", None)
    return jax.shard_map(
        functools.partial(local, mesh.shape["lat"], mesh.shape["lon"]),
        mesh=mesh,
        in_specs=(P("lat", "lon", None), rows, rows, rows, rows)
        + (P(), P(), P(), P(), P(), rows),
        out_specs=P("lat", "lon", None),
        check_vma=False,
    )
```

time: 81.4 us -> 29.7 us (0.36)
  Pallas kernels: 0 us -> 26.3 us
  starting transfers between devices: 26.3 us -> 0 us
  waiting for transfers between devices: 23 us -> 0 us
  between operations: 13.4 us -> 0.01 us
  matrix products: 10.8 us -> 0 us
  blocking collectives: 4.38 us -> 0 us
  other arithmetic: 1.99 us -> 0 us
  local copies, waits for them, and re-layouts: 1.17 us -> 3.15 us
    pallas_call x0 -> x1, Pallas kernels: none -> 26.3 us  [local(): pl.pallas_call(functools.partial(kernel, n_lat, n_lon, heads), out_shape=...]
    ppermute x9 -> x0, starting transfers between devices: 26.2 us -> none  [the longest x7 20.7 us: partner_2(): return lax.ppermute(block, axis, route)]
    ppermute x9 -> x0, waiting for transfers between devices: 21.1 us -> none  [the longest x7 19.9 us: partner_2(): return lax.ppermute(block, axis, route)]
    dot_general x9 -> x0, matrix products: 10.8 us -> none  [the longest x4 5.28 us: local(): jnp.dot(columns, piece_rows, preferred_element_type=jnp.float32)]
    all_gather x2 -> x0, blocking collectives: 4.38 us -> none  [the longest x1 2.19 us: local(): lax.all_gather(proj_bc, 'lon', axis=0, tiled=True)]
    unnamed x8 -> x2, local copies, waits for them, and re-layouts: 0.02 us -> 3.15 us
    all_gather x3 -> x0, waiting for transfers between devices: 1.15 us -> none  [the longest x1 1.1 us: local(): lax.all_gather(proj_x, 'lon', axis=0, tiled=True)]
  transfers between devices with their start and end apart: 12 -> 0, of which waited for: 7 -> 0; matrix products, arithmetic and copies ran while one was open for 14% -> 0% of each run, Pallas kernels for 0% -> 0%
where the time goes in v1:
time: 29.7 us; the launch traced here: 29.4 us
  Pallas kernels  26.3 us (89%)
  local copies, waits for them, and re-layouts  3.15 us (11%)
    pallas_call x1, Pallas kernels, local(): pl.pallas_call(functools.partial(kernel, n_lat, n_lon, heads), out_shape=...  26.3 us
    unnamed x2, local copies, waits for them, and re-layouts  3.15 us

profile of v1, /device:TPU:0, one launch (start us, length us, event | category | flops | bytes accessed | tf_op | source)
XLA Modules:
  0.0 29.4 jit_solution(10668370807508911508)
XLA Ops:
  0.0 1.5 %copy.12.wdt = bf16[512,16]{1,0:T(8,128)(2,1)} copy(bf16[512,16]{0,1:T(8,128)(2,1)} %param.15) | data formatting | bytes 32768 | tf_op args[4]
  1.5 26.3 %shard_map.109 = bf16[128,1024]{1,0:T(8,128)(2,1)} custom-call(bf16[128,1024]{1,0:T(8,128)(2,1)} %bitcast.6, bf16[512,1024]{1,0:T(8,128)(2,1)} %wx.1, bf16[512,1024]{1,0:T(8,128)(2,1)} %wz.1, bf16[512,128]{1,0:T(8,128)(2,1)} %wbc.1, bf16[512,16]{1,0:T(8,128)(2,1)} %copy.12.wdt, bf16[512,1024]{1,0:T(8,128)(2,1)} %wo.1, f32[4,1024]{1,0:T(4,128)} %cx.1, ...), custom_call_target="tpu_custom_call" | custom-call | tf_op jit(solution)/shard_map/pallas_call | solution.py:378
  27.8 1.7 %copy.14 = bf16[128,1,1024]{2,0,1:T(8,128)(2,1)} copy(bf16[128,1,1024]{2,0,1:T(8,128)(2,1)} %bitcast.5) | data formatting | bytes 524288

commit v2 on v1

--- a/solution.py
+++ b/solution.py
@@ -37,12 +37,17 @@
     wbc,
     wdt,
     wo,
+    cx_in,
+    cbc_in,
+    dtb_in,
+    lrate_in,
+    gain_in,
+    out,
     cx,
     cbc,
     dtb,
     lrate,
     gain,
-    out,
     fbuf,
     bx,
     bz,
@@ -78,7 +83,7 @@
     rows, width = fields.shape
     inner = wx.shape[1]
     state = wbc.shape[1] // 2
-    taps = cx.shape[0]
+    taps = cx_in.shape[0]
     kr = wx.shape[0]
     head_dim = inner // heads
     blocks = inner // LANES
@@ -102,6 +107,9 @@
     own = [pltpu.make_async_copy(fields, fbuf.at[pl.ds(HALO, rows)], local_sem.at[5])]
     for i, (src, dst) in enumerate(weights):
         own.append(pltpu.make_async_copy(src, dst.at[col], local_sem.at[i]))
+    small = ((cx_in, cx), (cbc_in, cbc), (dtb_in, dtb), (lrate_in, lrate), (gain_in, gain))
+    for i, (src, dst) in enumerate(small):
+        own.append(pltpu.make_async_copy(src, dst, local_sem.at[6 + i]))
     for c in own:
         c.start()
     pl.semaphore_wait(barrier, n_lat - 1 + n_lon - 1)
@@ -156,8 +164,22 @@
                 term = term.astype(bf16).astype(f32)
             acc[:, start : start + size] = term
 
+    def accumulate_dt(k):
+        source, columns = part(k)
+        term = lax.dot_general(
+            fbuf[HALO:, columns],
+            bdt[source],
+            (((1,), (1,)), ((), ())),
+            preferred_element_type=f32,
+        )
+        if k > 0:
+            term = term + accdt[...]
+        if k == n_lon - 1:
+            term = term.astype(bf16).astype(f32)
+        accdt[...] = term
+
     accumulate(0, bbc, accbc, 0, 256)
-    accumulate(0, bdt, accdt, HALO, 256)
+    accumulate_dt(0)
     accumulate(0, bx, accx, 0, 256)
 
     for k in range(1, n_lon):
@@ -165,7 +187,7 @@
         accumulate(k, bbc, accbc, 0, 256)
     for k in range(1, n_lon):
         arrived(1, k)
-        accumulate(k, bdt, accdt, HALO, 256)
+        accumulate_dt(k)
 
     def conv(acc, kernel_ref, start, size):
         total = None
@@ -216,7 +238,9 @@
     trecv[me] = tbuf[me]
 
     def exchange(k, buf, dst, send, recv):
-        to = lax.rem(me + k, n_lat)
+        return outgoing(lax.rem(me + k, n_lat), buf, dst, send, recv)
+
+    def outgoing(to, buf, dst, send, recv):
         return pltpu.make_async_remote_copy(
             src_ref=buf.at[to],
             dst_ref=dst.at[me],
@@ -255,14 +279,14 @@
         weighted = (block.astype(f32) * end_weight[:, lanes]).astype(bf16)
         end_state = jnp.dot(bc_t, weighted, preferred_element_type=f32)
         for r in range(split):
-            sbuf[r * blocks + c] = end_state[r * piece : (r + 1) * piece, :].astype(bf16)
+            to = r * blocks + c
+            sbuf[to] = end_state[r * piece : (r + 1) * piece, :].astype(bf16)
+
+            @pl.when(me != to)
+            def _():
+                outgoing(to, sbuf, srecv, s_send, s_recv).start()
+
     srecv[me] = sbuf[me]
-
-    def send_s(k, carry):
-        exchange(k, sbuf, srecv, s_send, s_recv).start()
-        return carry
-
-    lax.fori_loop(1, n_lat, send_s, 0)
 
     half = lax.broadcasted_iota(jnp.int32, (rows, LANES), 1) // head_dim
     for c in range(blocks):
@@ -287,14 +311,13 @@
             incoming(d, sbuf, srecv, s_send, s_recv).wait_recv()
 
         pbuf[d] = carried.astype(bf16)
+
+        @pl.when(me != d)
+        def _():
+            outgoing(d, pbuf, precv, p_send, p_recv).start()
+
         carried = trecv[d][0:1, :] * carried + srecv[d].astype(f32)
     precv[me] = pbuf[me]
-
-    def send_p(k, carry):
-        exchange(k, pbuf, precv, p_send, p_recv).start()
-        return carry
-
-    lax.fori_loop(1, n_lat, send_p, 0)
 
     accumulate(0, bz, accz, HALO, 256)
     for k in range(1, n_lon):
@@ -372,20 +395,38 @@
     kr, inner = proj_x.shape
     state = proj_bc.shape[1] // 2
     piece = state * inner // LANES // n_lat
-    any_spec = pl.BlockSpec(memory_space=pl.ANY)
+    operands = (
+        fields.reshape(rows * cols, width),
+        proj_x,
+        proj_z,
+        proj_bc,
+        proj_dt.T,
+        proj_out,
+        conv_x,
+        conv_bc,
+        dt_bias.reshape(1, -1),
+        log_rate.reshape(1, -1),
+        norm_gain.reshape(1, -1),
+    )
+    hbm = pl.BlockSpec(memory_space=pl.ANY)
     vmem = pl.BlockSpec(memory_space=pltpu.VMEM)
     dma = pltpu.SemaphoreType.DMA
     out = pl.pallas_call(
         functools.partial(kernel, n_lat, n_lon, heads),
         out_shape=jax.ShapeDtypeStruct((rows * cols, width), bf16),
-        in_specs=[any_spec] * 6 + [vmem] * 5,
+        in_specs=[hbm] * 11,
         out_specs=vmem,
         scratch_shapes=[
+            pltpu.VMEM(conv_x.shape, f32),
+            pltpu.VMEM(conv_bc.shape, f32),
+            pltpu.VMEM((1, heads), f32),
+            pltpu.VMEM((1, heads), f32),
+            pltpu.VMEM((1, inner), f32),
             pltpu.VMEM((HALO + rows, width), bf16),
             pltpu.VMEM((n_lon, kr, inner), bf16),
             pltpu.VMEM((n_lon, kr, inner), bf16),
             pltpu.VMEM((n_lon, kr, 2 * state), bf16),
-            pltpu.VMEM((n_lon, kr, heads), bf16),
+            pltpu.VMEM((n_lon, heads, kr), bf16),
             pltpu.VMEM((n_lon,) + proj_out.shape, bf16),
             pltpu.VMEM((HALO + rows, inner), f32),
             pltpu.VMEM((rows, inner), f32),
@@ -401,7 +442,7 @@
             pltpu.VMEM((n_lat, piece, LANES), bf16),
             pltpu.VMEM((n_lat, piece, LANES), bf16),
             pltpu.VMEM((n_lat, piece, LANES), bf16),
-            dma((6,)),
+            dma((11,)),
             dma((5, n_lon)),
             dma((5, n_lon)),
             dma,
@@ -409,20 +450,10 @@
         ]
         + [dma((n_lat,))] * 6,
         compiler_params=pltpu.CompilerParams(
-            collective_id=0, has_side_effects=True, vmem_limit_bytes=56 * 1024 * 1024
+            collective_id=0, has_side_effects=True, vmem_limit_bytes=16 * 1024 * 1024
         ),
     )(
-        fields.reshape(rows * cols, width),
-        proj_x,
-        proj_z,
-        proj_bc,
-        proj_dt,
-        proj_out,
-        conv_x,
-        conv_bc,
-        dt_bias.reshape(1, -1),
-        log_rate.reshape(1, -1),
-        norm_gain.reshape(1, -1),
+        *(pltpu.with_memory_space_constraint(v, pltpu.HBM) for v in operands)
     )
     return out.reshape(rows, cols, width)
 

time: 29.7 us -> 25.6 us (0.86)
  local copies, waits for them, and re-layouts: 3.15 us -> 0.71 us
  Pallas kernels: 26.3 us -> 24.7 us
    unnamed x2 -> x1, local copies, waits for them, and re-layouts: 3.15 us -> 0.71 us
    pallas_call x1, Pallas kernels: 26.3 us -> 24.7 us  [local(): pl.pallas_call(functools.partial(kernel, n_lat, n_lon, heads), out_shape=...]
where the time goes in v2:
time: 25.6 us; the launch traced here: 25.4 us
  Pallas kernels  24.7 us (96%)
  local copies, waits for them, and re-layouts  0.71 us (3%)
    pallas_call x1, Pallas kernels, local(): pl.pallas_call(functools.partial(kernel, n_lat, n_lon, heads), out_shape=...  24.7 us
    unnamed x1, local copies, waits for them, and re-layouts  0.71 us

profile of v2, /device:TPU:0, one launch (start us, length us, event | category | flops | bytes accessed | tf_op | source)
XLA Modules:
  0.0 25.4 jit_solution(14054224969838116753)
XLA Ops:
  0.0 24.7 %shard_map.109 = bf16[128,1024]{1,0:T(8,128)(2,1)S(1)} custom-call(bf16[128,1024]{1,0:T(8,128)(2,1)} %bitcast.7, bf16[512,1024]{1,0:T(8,128)(2,1)} %wx.1, bf16[512,1024]{1,0:T(8,128)(2,1)} %wz.1, bf16[512,128]{1,0:T(8,128)(2,1)} %wbc.1, bf16[16,512]{1,0:T(8,128)(2,1)} %bitcast.8, bf16[512,1024]{1,0:T(8,128)(2,1)} %wo.1, f32[4,1024]{1,0:T(4,128)} %cx_in.1, ...), custom_call_target="tpu_custom_call" | custom-call | tf_op jit(solution)/shard_map/pallas_call | solution.py:414
  24.7 0.7 %copy.13 = bf16[128,1,1024]{2,0,1:T(8,128)(2,1)} copy(bf16[128,1,1024]{2,0,1:T(8,128)(2,1)S(1)} %bitcast.6) | data formatting | bytes 524288

commit v3 on v2

--- a/solution.py
+++ b/solution.py
@@ -203,8 +203,6 @@
     lane = lax.broadcasted_iota(jnp.int32, (rows, 2 * state), 1)
     bc16 = bc_act.astype(bf16)
     bc_f = bc16.astype(f32)
-    read = pltpu.roll(bc_f, state, 1).astype(bf16)
-    b_only = jnp.where(lane < state, bc_f, 0.0).astype(bf16)
     bc_t = bc_f.T.astype(bf16)
 
     prm[...] = jnp.zeros_like(prm)
@@ -222,8 +220,7 @@
         jnp.where(causal, 1.0, 0.0), log_step, precision=highest, preferred_element_type=f32
     )
     dec[0] = cum
-    dec[1] = cum.T
-    dec[2] = step_dt.T
+    dec[1] = step_dt
     band_total = cum[rows - 1 : rows, :]
     spread = jnp.where(
         lax.broadcasted_iota(jnp.int32, (LANES, inner), 1) // head_dim
@@ -264,9 +261,6 @@
 
     lax.fori_loop(1, n_lat, send_t, 0)
 
-    scores = lax.dot_general(
-        read, b_only, (((1,), (1,)), ((), ())), preferred_element_type=f32
-    )
     end_weight = expand(jnp.exp(band_total - cum) * step_dt, spread)
 
     for k in range(1, n_lon):
@@ -288,6 +282,13 @@
 
     srecv[me] = sbuf[me]
 
+    read = pltpu.roll(bc_f, state, 1).astype(bf16)
+    b_only = jnp.where(lane < state, bc_f, 0.0).astype(bf16)
+    scores = lax.dot_general(
+        read, b_only, (((1,), (1,)), ((), ())), preferred_element_type=f32
+    )
+    dec[2] = dec[1].T
+    dec[1] = dec[0].T
     half = lax.broadcasted_iota(jnp.int32, (rows, LANES), 1) // head_dim
     for c in range(blocks):
         lanes = slice(c * LANES, (c + 1) * LANES)
@@ -300,7 +301,7 @@
             term = jnp.dot(mix, act[:, lanes], preferred_element_type=f32)
             mixed = term if mixed is None else jnp.where(half == g, term, mixed)
         diag[:, lanes] = mixed
-    start_decay = jnp.exp(cum)
+    start_decay = jnp.exp(dec[0])
 
     carried = jnp.zeros((piece, LANES), f32)
     for d in range(n_lat):
@@ -343,13 +344,10 @@
         lower = jnp.concatenate([jnp.zeros_like(prefix), prefix], axis=0)
         y = jnp.dot(bc16, lower, preferred_element_type=f32) * accx[0:rows, lanes] + diag[:, lanes]
         gated = y * accz[:, lanes]
-        diag[:, lanes] = gated
+        act[:, lanes] = (gated * gain[:, lanes]).astype(bf16)
         square = square + gated * gated
     mean = jnp.sum(square, axis=1, keepdims=True) * (1.0 / inner)
     scale = lax.rsqrt(mean + norm_epsilon)
-    for c in range(blocks):
-        lanes = slice(c * LANES, (c + 1) * LANES)
-        act[:, lanes] = (diag[:, lanes] * scale * gain[:, lanes]).astype(bf16)
     for start in range(0, width, 256):
         total = None
         for s in range(n_lon):
@@ -359,7 +357,7 @@
                 preferred_element_type=f32,
             )
             total = term if total is None else total + term
-        out[:, start : start + 256] = total.astype(bf16)
+        out[:, start : start + 256] = (total * scale).astype(bf16)
 
     halo.wait_send()
     for i in range(5):

time: 25.6 us -> 25.6 us (level)
  no operation moved by 1% of the time
where the time goes in v3:
time: 25.6 us; the launch traced here: 25.5 us
  Pallas kernels  24.8 us (97%)
  local copies, waits for them, and re-layouts  0.71 us (3%)
    pallas_call x1, Pallas kernels, local(): pl.pallas_call(functools.partial(kernel, n_lat, n_lon, heads), out_shape=...  24.8 us
    unnamed x1, local copies, waits for them, and re-layouts  0.71 us

profile of v3, /device:TPU:0, one launch (start us, length us, event | category | flops | bytes accessed | tf_op | source)
XLA Modules:
  0.0 25.5 jit_solution(5420977413669407659)
XLA Ops:
  0.0 24.8 %shard_map.109 = bf16[128,1024]{1,0:T(8,128)(2,1)S(1)} custom-call(bf16[128,1024]{1,0:T(8,128)(2,1)} %bitcast.7, bf16[512,1024]{1,0:T(8,128)(2,1)} %wx.1, bf16[512,1024]{1,0:T(8,128)(2,1)} %wz.1, bf16[512,128]{1,0:T(8,128)(2,1)} %wbc.1, bf16[16,512]{1,0:T(8,128)(2,1)} %bitcast.8, bf16[512,1024]{1,0:T(8,128)(2,1)} %wo.1, f32[4,1024]{1,0:T(4,128)} %cx_in.1, ...), custom_call_target="tpu_custom_call" | custom-call | tf_op jit(solution)/shard_map/pallas_call | solution.py:412
  24.8 0.7 %copy.13 = bf16[128,1,1024]{2,0,1:T(8,128)(2,1)} copy(bf16[128,1,1024]{2,0,1:T(8,128)(2,1)S(1)} %bitcast.6) | data formatting | bytes 524288
